TPU v7x, 256 devices: a whole 4x4x8 slice. The times are simulated.
256 devices in a mesh: dp: 128 (over z, x, y_hi, core), tensor: 2 (over y_lo).
Axes of the slice: x: 4, y: 4 (y_hi: 2, y_lo: 2; y = y_hi * 2 + y_lo), z: 8, core: 2. Of those that a mesh axis runs over, the one named last changes fastest.
Arguments:
- tokens: bfloat16 [16384, 2048], P('dp'), may hold values from -16 to 16
- teacher: bfloat16 [16384, 2048], P('dp'), may hold values from -6 to 6
- inner_weight: float32 [2048, 512], P('dp', 'tensor'), may hold values from -0.125 to 0.125
- output_weight: bfloat16 [2048, 2048], P('dp', 'tensor'), may hold values from -0.125 to 0.125
- inner_first: float32 [2048, 512], P('dp', 'tensor'), may hold values from -2 to 2
- inner_second: float32 [2048, 512], P('dp', 'tensor'), may hold values from 0.2 to 2
- state_weight: bfloat16 [2048, 32], replicated, may hold values from -0.03125 to 0.03125
- step_weight: bfloat16 [2048, 16], P(None, 'tensor'), may hold values from -0.0390625 to 0.0390625
- step_bias: float32 [16], P('tensor'), may hold values from -4 to 0
- decay_log: float32 [16], P('tensor'), may hold values from -3 to 1
- skip_gain: float32 [16], P('tensor'), may hold values from 0.5 to 1.5
Outputs:
- distill_loss: float32 [], replicated
- inner_update: float32 [2048, 512], P('dp', 'tensor')
- inner_first_next: float32 [2048, 512], P('dp', 'tensor')
- inner_second_next: float32 [2048, 512], P('dp', 'tensor')
All inputs are finite; a program needn't handle non-finite values.
Results may differ from a plain program's by a relative error of at most 0.0016.
Values may be sent and summed in bfloat16 or wider, within the bound.
A program may use at most 64 MiB of HBM per device.

v0:
```python
import jax
import jax.numpy as jnp
from jax import lax
from jax.sharding import Mesh
from jax.sharding import PartitionSpec as P

HEADS = 16
GROUPS = 4
HEAD_DIM = 128
STEP = 20
DP = ("dp_0", "dp_1", "dp_2", "dp_3")
DP_TENSOR = ("dp_0", "dp_1", "dp_2", "dp_3", "tensor")
beta_one = 0.9
beta_two = 0.95
adam_eps = 1e-08
weight_decay = 0.1
norm_eps = 1e-06


def sent_together(arrays, axis, dim, along):
    widths = [a.shape[along] for a in arrays]
    both = jnp.concatenate(arrays, axis=along)
    whole = lax.all_gather(both, axis, axis=dim, tiled=True)
    return tuple(jnp.split(whole, [sum(widths[:k]) for k in range(1, len(widths))], axis=along))


def sent_to_all(x, axis):
    peers = lax.axis_size(axis)
    return lax.all_to_all(jnp.broadcast_to(x[None], (peers, *x.shape)), axis, 0, 0, tiled=True)


def of_everyone(x, axis):
    everything = sent_to_all(x, axis)
    return jnp.sum(everything, axis=0)


def cut_along(x, dim, peers):
    before, after = (x.shape[:dim], x.shape[dim + 1 :])
    return jnp.moveaxis(x.reshape(*before, peers, -1, *after), dim, 0)


def sum_at_owner(x, axis, dim):
    peers = lax.axis_size(axis)
    pieces = lax.all_to_all(cut_along(x, dim, peers), axis, 0, 0, tiled=True)
    return jnp.sum(pieces, axis=0)


def sum_in_two_steps(x, axes, dim):
    far, near = axes
    own = sum_at_owner(cut_along(x, dim, lax.axis_size(far)), near, dim + 1)
    return jnp.sum(lax.all_to_all(own, far, 0, 0, tiled=True), axis=0)


def one_axis_at_a_time(x, axes):
    for axis in axes:
        x = lax.psum(x, axis)
    return x


def mixing(sequence, state_weight, step_weight, step_bias, decay_log):
    state_width = state_weight.shape[1] // 2
    projected = jnp.dot(sequence, state_weight, preferred_element_type=jnp.float32)
    b_coef = projected[:, :state_width]
    c_coef = projected[:, state_width:]
    gram_matrix = jnp.dot(c_coef, b_coef.T, precision=lax.Precision.HIGHEST)
    step_size = jax.nn.softplus(
        jnp.dot(sequence, step_weight, preferred_element_type=jnp.float32) + step_bias
    )
    rate_step = jnp.exp(decay_log) * step_size
    cumulative = jnp.cumsum(rate_step, axis=0).T
    length = sequence.shape[0]
    row_later = lax.broadcasted_iota(jnp.int32, (length, length), 0)
    earlier = lax.broadcasted_iota(jnp.int32, (length, length), 1)
    causal = row_later >= earlier
    log_decay = cumulative[:, None, :] - cumulative[:, :, None]
    decay_matrix = jnp.where(causal[None], jnp.exp(jnp.minimum(log_decay, 0.0)), 0.0)
    return (gram_matrix[None] * decay_matrix * step_size.T[:, None, :]).astype(jnp.bfloat16)


def contract_rows(left, right):
    return lax.dot_general(
        left, right, (((0,), (0,)), ((), ())), preferred_element_type=jnp.float32
    )


def on_device(
    tokens,
    teacher,
    inner_weight,
    output_weight,
    inner_first,
    inner_second,
    state_weight,
    step_weight,
    step_bias,
    decay_log,
    skip_gain,
):
    seq_rows, model_width = tokens.shape
    heads_here = step_weight.shape[1]
    groups_here = inner_weight.shape[1] // HEAD_DIM
    ratio = HEADS // GROUPS
    total_tokens = seq_rows * lax.axis_size(DP)
    inner_full, output_full = sent_together(
        (inner_weight.astype(jnp.bfloat16), output_weight), DP, 0, 1
    )
    weights_mix = mixing(tokens, state_weight, step_weight, step_bias, decay_log)
    projected = jnp.dot(tokens, inner_full, preferred_element_type=jnp.float32).astype(jnp.bfloat16)
    heads_in = jnp.repeat(projected.reshape(seq_rows, groups_here, HEAD_DIM), ratio, axis=1)
    mixed = jnp.einsum(
        "hts,shp->thp", weights_mix, heads_in, preferred_element_type=jnp.float32
    ) + skip_gain[None, :, None] * heads_in.astype(jnp.float32)
    inner = mixed.astype(jnp.bfloat16).reshape(seq_rows, heads_here * HEAD_DIM)
    partial_out = lax.dot_general(
        inner, output_full, (((1,), (1,)), ((), ())), preferred_element_type=jnp.float32
    )
    student = of_everyone(partial_out, "tensor")
    error_rows = student - teacher.astype(jnp.float32)
    square_sum = jnp.where(lax.axis_index("tensor") == 0, jnp.sum(error_rows * error_rows), 0.0)
    grad_out = error_rows.astype(jnp.bfloat16)
    grad_inner = jnp.dot(grad_out, output_full, preferred_element_type=jnp.float32).astype(
        jnp.bfloat16
    )
    grad_heads = grad_inner.reshape(seq_rows, heads_here, HEAD_DIM)
    back = jnp.einsum(
        "hts,thp->shp", weights_mix, grad_heads, preferred_element_type=jnp.float32
    ) + skip_gain[None, :, None] * grad_heads.astype(jnp.float32)
    grouped = jnp.sum(back.reshape(seq_rows, groups_here, ratio, HEAD_DIM), axis=2)
    grad_projected = grouped.astype(jnp.bfloat16).reshape(seq_rows, groups_here * HEAD_DIM)
    inner_grad = sum_in_two_steps(
        contract_rows(tokens, grad_projected), (("dp_0", "dp_1", "dp_2"), "dp_3"), 0
    )
    local_squares = jnp.sum(inner_grad * inner_grad)
    squares_total, error_total = (
        one_axis_at_a_time(local_squares, DP_TENSOR),
        one_axis_at_a_time(square_sum, DP_TENSOR),
    )
    entry_count = model_width * groups_here * HEAD_DIM * lax.axis_size("tensor")
    root_mean = jnp.sqrt(squares_total / entry_count)
    factor = jnp.minimum(1.0, 1.0 / (root_mean + norm_eps))
    distill_loss = error_total / (total_tokens * model_width)
    first_fix = 1.0 - beta_one**STEP
    second_fix = 1.0 - beta_two**STEP
    clipped = factor * inner_grad
    first_next = beta_one * inner_first + (1.0 - beta_one) * clipped
    second_next = beta_two * inner_second + (1.0 - beta_two) * clipped * clipped
    update = (
        first_next / first_fix / (jnp.sqrt(second_next / second_fix) + adam_eps)
        + weight_decay * inner_weight
    )
    return (distill_loss, update, first_next, second_next)


def solution(mesh):
    finer = Mesh(
        mesh.devices.reshape(8, 4, 2, 2, mesh.shape["tensor"]),
        ("dp_0", "dp_1", "dp_2", "dp_3", "tensor"),
    )
    return jax.shard_map(
        on_device,
        mesh=finer,
        in_specs=(
            P(DP, None),
            P(DP, None),
            P(DP, "tensor"),
            P(DP, "tensor"),
            P(DP, "tensor"),
            P(DP, "tensor"),
            P(),
            P(None, "tensor"),
            P("tensor"),
            P("tensor"),
            P("tensor"),
        ),
        out_specs=(P(), P(DP, "tensor"), P(DP, "tensor"), P(DP, "tensor")),
        check_vma=False,
    )
```

profile of v0, /device:TPU:1, one launch (start us, length us, event | category | flops | bytes accessed | tf_op | source)
XLA Modules:
  0.0 278.1 jit_solution(4933198831317484721)
XLA Ops:
  7.2 0.0 copy-start
  7.2 0.0 all-gather.2.cloned.1.call-start
  7.2 0.8 convert_element_type.37
  8.0 1.4 pad_maximum_fusion
  9.4 0.0 all-gather.2.cloned.1.call-update
  9.4 0.7 exp.13
  10.1 0.0 copy-done
  10.1 1.0 compare_select_fusion
  11.1 0.1 fusion.17
  11.2 0.1 copy.30
  11.3 0.2 reduce_window_sum.11
  11.5 1.2 fusion.25
  12.7 0.3 fusion.14
  13.0 124.1 %all-gather.2.cloned.1.call-done = bf16[2048,1280]{1,0:T(8,128)(2,1)} async-done(((bf16[16,1280]{1,0:T(8,128)(2,1)}), bf16[2048,1280]{1,0:T(8,128)(2,1)}) %all-gather.2.cloned.1.call-update) | async-done | bytes 5242896 | tf_op jit(solution)/shard_map/all_gather | solution.py:23
  137.1 1.7 convolution_convert_fusion
  138.9 1.0 fusion.9
  139.9 3.7 %fusion.2 = f32[128,2048]{1,0:T(8,128)S(1)} fusion(bf16[128,1024]{0,1:T(8,128)(2,1)S(1)} %bitcast.59, bf16[2048,1280]{1,0:T(8,128)(2,1)} %all-gather.2.cloned.1.call-done), kind=kOutput, calls=%fused_computation.2 | convolution fusion | flops 536870912 | bytes 5505024 | tf_op jit(solution)/shard_map/dot_general | solution.py:114
  143.6 0.2 broadcast_in_dim.16
  143.9 0.0 copy-start.1
  143.9 27.3 %all_to_all.15 = f32[2,128,2048]{2,1,0:T(8,128)S(1)} all-to-all(f32[2,128,2048]{2,1,0:T(8,128)S(1)} %broadcast_in_dim.16), channel_id=1, replica_groups=mesh['dp_0'=8,'dp_1'=4,'dp_2'=2,'dp_3'=2,'tensor'=2] {'tensor'}, dimensions={0} | all-to-all | bytes 4194304 | tf_op jit(solution)/shard_map/all_to_all | solution.py:29
  171.2 1.2 reduce_sum.54
  172.5 0.0 copy-done.1
  172.5 3.2 %fusion.6 = bf16[128,1024]{1,0:T(8,128)(2,1)S(1)} fusion(bf16[2048,1280]{1,0:T(8,128)(2,1)} %all-gather.2.cloned.1.call-done, f32[128,2048]{1,0:T(8,128)} %reduce_sum.54, bf16[128,2048]{1,0:T(8,128)(2,1)S(1)} %copy-done.1), kind=kOutput, calls=%fused_computation.9 | convolution fusion | flops 537788416 | bytes 6029312 | tf_op jit(solution)/shard_map/dot_general | solution.py:121
  175.7 0.2 copy.33
  175.9 0.0 copy-done.5
  175.9 0.4 bitcast_reduce_fusion
  176.3 0.4 convolution_bitcast_fusion
  176.7 1.9 copy.34
  178.6 1.8 copy.35
  180.4 6.2 %all_to_all.16 = f32[2,64,16,256]{3,2,1,0:T(8,128)S(1)} all-to-all(f32[2,64,16,256]{3,2,1,0:T(8,128)S(1)} %copy.35), channel_id=1, replica_groups=mesh['dp_0'=8,'dp_1'=4,'dp_2'=2,'dp_3'=2,'tensor'=2] {'dp_3'}, dimensions={0} | all-to-all | bytes 4194304 | tf_op jit(solution)/shard_map/all_to_all | solution.py:44
  186.6 0.0 copy-start.2
  186.6 0.0 copy-start.3
  186.6 0.0 copy-start.4
  186.6 1.3 reduce_sum.57
  187.8 7.8 %all-to-all-start.2 = ((f32[64,16,256]{2,1,0:T(8,128)}), f32[64,16,256]{2,1,0:T(8,128)S(1)}, u32[]{:S(2)}, u32[]{:S(2)}) async-start(f32[64,16,256]{2,1,0:T(8,128)} %reduce_sum.57), calls=%async_computation.2 | async-start | bytes 2097152 | tf_op jit(solution)/shard_map/all_to_all | solution.py:51
  195.7 2.1 multiply_reduce_fusion
  198.4 25.0 %all-to-all-done.2 = f32[64,16,256]{2,1,0:T(8,128)S(1)} async-done(((f32[64,16,256]{2,1,0:T(8,128)}), f32[64,16,256]{2,1,0:T(8,128)S(1)}, u32[]{:S(2)}, u32[]{:S(2)}) %all-to-all-start.2) | async-done | bytes 1048608 | tf_op jit(solution)/shard_map/all_to_all | solution.py:51
  223.4 0.1 reduce_sum.58
  223.5 0.6 multiply_reduce_fusion.1
  224.1 14.2 %all-reduce = (f32[]{:T(128)}, f32[]{:T(128)}) all-reduce(f32[]{:T(128)S(6)} %select_n.18, f32[]{:T(128)} %multiply_reduce_fusion.1), channel_id=1, replica_groups=mesh['dp_0'=8,'dp_1'=4,'dp_2'=2,'dp_3'=2,'tensor'=2] {'dp_0'}, use_global_device_ids=true, to_apply=%region_3.4 | all-reduce | flops 2 | bytes 16 | tf_op jit(solution)/shard_map/psum | solution.py:56
  238.3 7.5 %all-reduce.1 = (f32[]{:T(128)}, f32[]{:T(128)}) all-reduce(f32[]{:T(128)} %get-tuple-element.4, f32[]{:T(128)} %get-tuple-element.5), channel_id=1, replica_groups=mesh['dp_0'=8,'dp_1'=4,'dp_2'=2,'dp_3'=2,'tensor'=2] {'dp_1'}, use_global_device_ids=true, to_apply=%region_4.5 | all-reduce | flops 2 | bytes 16 | tf_op jit(solution)/shard_map/psum | solution.py:56
  245.8 5.9 %all-reduce.4 = (f32[]{:T(128)}, f32[]{:T(128)}) all-reduce(f32[]{:T(128)} %get-tuple-element.6, f32[]{:T(128)} %get-tuple-element.7), channel_id=1, replica_groups=mesh['dp_0'=8,'dp_1'=4,'dp_2'=2,'dp_3'=2,'tensor'=2] {'dp_2'}, use_global_device_ids=true, to_apply=%region_5.6 | all-reduce | flops 2 | bytes 16 | tf_op jit(solution)/shard_map/psum | solution.py:56
  251.7 11.9 %all-reduce.3 = (f32[]{:T(128)}, f32[]{:T(128)}) all-reduce(f32[]{:T(128)} %get-tuple-element.12, f32[]{:T(128)} %get-tuple-element.13), channel_id=1, replica_groups=mesh['dp_0'=8,'dp_1'=4,'dp_2'=2,'dp_3'=2,'tensor'=2] {'dp_3'}, use_global_device_ids=true, to_apply=%region_6.7 | all-reduce | flops 2 | bytes 16 | tf_op jit(solution)/shard_map/psum | solution.py:56
  263.6 4.4 %all-reduce.2 = (f32[]{:T(128)}, f32[]{:T(128)}) all-reduce(f32[]{:T(128)} %get-tuple-element.10, f32[]{:T(128)} %get-tuple-element.11), channel_id=1, replica_groups=mesh['dp_0'=8,'dp_1'=4,'dp_2'=2,'dp_3'=2,'tensor'=2] {'tensor'}, use_global_device_ids=true, to_apply=%region_7.8 | all-reduce | flops 2 | bytes 16 | tf_op jit(solution)/shard_map/psum | solution.py:56
  269.4 0.0 copy-done.2
  269.4 0.0 copy-done.3
  269.4 0.0 copy-done.4
  269.4 0.6 multiply_add_fusion
  (4 shorter events, 0.1 us)
Async XLA Ops:
  7.2 2.9 %copy-start = (bf16[128,2048]{1,0:T(8,128)(2,1)S(1)}, bf16[128,2048]{1,0:T(8,128)(2,1)}, u32[]{:S(2)}) copy-start(bf16[128,2048]{1,0:T(8,128)(2,1)} %param.11) | copy-start | bytes 1572868
  7.2 129.9 %all-gather.2.cloned.1.call-start = ((), (), s32[]{:S(2)}) async-start(), calls=%async_computation.3 | async-start | bytes 5283840 | tf_op jit(solution)/shard_map/all_gather | solution.py:23
  143.9 28.6 %copy-start.1 = (bf16[128,2048]{1,0:T(8,128)(2,1)S(1)}, bf16[128,2048]{1,0:T(8,128)(2,1)}, u32[]{:S(2)}) copy-start(bf16[128,2048]{1,0:T(8,128)(2,1)} %param.12) | copy-start | bytes 1572868
  172.5 3.4 %copy-start.5 = (f32[8]{0:T(128)S(1)}, f32[8]{0:T(128)}, u32[]{:S(2)}) copy-start(f32[8]{0:T(128)} %param.21) | copy-start | bytes 100
  186.6 82.9 %copy-start.2 = (f32[16,256]{1,0:T(8,128)S(1)}, f32[16,256]{1,0:T(8,128)}, u32[]{:S(2)}) copy-start(f32[16,256]{1,0:T(8,128)} %param.13) | copy-start | bytes 49156
  186.6 82.9 %copy-start.3 = (f32[16,256]{1,0:T(8,128)S(1)}, f32[16,256]{1,0:T(8,128)}, u32[]{:S(2)}) copy-start(f32[16,256]{1,0:T(8,128)} %param.15) | copy-start | bytes 49156
  186.6 82.9 %copy-start.4 = (f32[16,256]{1,0:T(8,128)S(1)}, f32[16,256]{1,0:T(8,128)}, u32[]{:S(2)}) copy-start(f32[16,256]{1,0:T(8,128)} %param.16) | copy-start | bytes 49156
  187.8 35.6 %all-to-all-start.2 = ((f32[64,16,256]{2,1,0:T(8,128)}), f32[64,16,256]{2,1,0:T(8,128)S(1)}, u32[]{:S(2)}, u32[]{:S(2)}) async-start(f32[64,16,256]{2,1,0:T(8,128)} %reduce_sum.57), calls=%async_computation.2 | async-start | bytes 2097152 | tf_op jit(solution)/shard_map/all_to_all | solution.py:51
Sparse Core Ops, SparseCore 0:
  11.6 125.4 all-gather.1
where the time goes:
time: 279 us; the launch traced here: 278 us
  waiting for transfers between devices  149 us (53%)
  blocking collectives  77.4 us (28%)
  between operations  17.4 us (6%)
  matrix products  13 us (5%)
  other arithmetic  8.35 us (3%)
  starting transfers between devices  7.89 us (3%)
  local copies, waits for them, and re-layouts  4.93 us (2%)
    all_gather x1, waiting for transfers between devices, sent_together(): whole = lax.all_gather(both, axis, axis=dim, tiled=True)  124 us
    psum x5, blocking collectives, one_axis_at_a_time(): x = lax.psum(x, axis)  43.9 us
    all_to_all x1, blocking collectives, sent_to_all(): lax.all_to_all(jnp.broadcast_to(x[None], (peers, *x.shape)), axis, 0, 0,...  27.3 us
    all_to_all x1, waiting for transfers between devices, sum_in_two_steps(): return jnp.sum(lax.all_to_all(own, far, 0, 0, tiled=True), axis=0)  25 us
    all_to_all x1, starting transfers between devices, sum_in_two_steps(): return jnp.sum(lax.all_to_all(own, far, 0, 0, tiled=True), axis=0)  7.85 us
    all_to_all x1, blocking collectives, sum_at_owner(): pieces = lax.all_to_all(cut_along(x, dim, peers), axis, 0, 0, tiled=True)  6.16 us
  transfers between devices with their start and end apart: 2, of which 2 were waited for; matrix products, arithmetic and copies ran while one was open for 2% of the time, Pallas kernels for 0%

commit v1 on v0

--- a/solution.py
+++ b/solution.py
@@ -53,7 +53,7 @@
 
 def one_axis_at_a_time(x, axes):
     for axis in axes:
-        x = lax.psum(x, axis)
+        x = jax.lax.all_gather(x, axis).sum(axis=0)
     return x
 
 

time: 279 us -> 297 us (1.065)
  local copies, waits for them, and re-layouts: 4.93 us -> 21.3 us
  other arithmetic: 8.35 us -> 14.4 us
  blocking collectives: 77.4 us -> 74.3 us
    psum x5 -> x0, blocking collectives: 43.9 us -> none  [one_axis_at_a_time(): x = lax.psum(x, axis)]
    unnamed x0 -> x5, blocking collectives: none -> 40.8 us
    unnamed x12 -> x47, local copies, waits for them, and re-layouts: 0.03 us -> 16.4 us
    reduce_sum x0 -> x10, other arithmetic: none -> 6.01 us  [one_axis_at_a_time(): x = jax.lax.all_gather(x, axis).sum(axis=0)]
where the time goes in v1:
time: 297 us; the launch traced here: 296 us
  waiting for transfers between devices  148 us (50%)
  blocking collectives  74.3 us (25%)
  local copies, waits for them, and re-layouts  21.3 us (7%)
  between operations  17.4 us (6%)
  other arithmetic  14.4 us (5%)
  matrix products  13 us (4%)
  starting transfers between devices  7.89 us (3%)
    all_gather x1, waiting for transfers between devices, sent_together(): whole = lax.all_gather(both, axis, axis=dim, tiled=True)  124 us
    unnamed x5, blocking collectives  40.8 us
    all_to_all x1, blocking collectives, sent_to_all(): lax.all_to_all(jnp.broadcast_to(x[None], (peers, *x.shape)), axis, 0, 0,...  27.3 us
    all_to_all x1, waiting for transfers between devices, sum_in_two_steps(): return jnp.sum(lax.all_to_all(own, far, 0, 0, tiled=True), axis=0)  23.6 us
    unnamed x47, local copies, waits for them, and re-layouts  16.4 us
    all_to_all x1, starting transfers between devices, sum_in_two_steps(): return jnp.sum(lax.all_to_all(own, far, 0, 0, tiled=True), axis=0)  7.85 us
    all_to_all x1, blocking collectives, sum_at_owner(): pieces = lax.all_to_all(cut_along(x, dim, peers), axis, 0, 0, tiled=True)  6.16 us
    reduce_sum x10, other arithmetic, one_axis_at_a_time(): x = jax.lax.all_gather(x, axis).sum(axis=0)  6.01 us
  transfers between devices with their start and end apart: 2, of which 2 were waited for; matrix products, arithmetic and copies ran while one was open for 2% of the time, Pallas kernels for 0%

profile of v1, /device:TPU:1, one launch (start us, length us, event | category | flops | bytes accessed | tf_op | source)
XLA Modules:
  0.0 295.9 jit_solution(9022115795669282368)
XLA Ops:
  7.2 0.8 convert_element_type.37
  8.0 1.4 pad_maximum_fusion
  9.4 0.7 exp.13
  10.1 1.0 compare_select_fusion
  11.5 1.2 fusion.25
  13.0 124.1 %all-gather.2.cloned.1.call-done = bf16[2048,1280]{1,0:T(8,128)(2,1)} async-done(((bf16[16,1280]{1,0:T(8,128)(2,1)}), bf16[2048,1280]{1,0:T(8,128)(2,1)}) %all-gather.2.cloned.1.call-update) | async-done | bytes 5242896 | tf_op jit(solution)/shard_map/all_gather | solution.py:23
  137.1 1.7 convolution_convert_fusion
  138.9 1.0 fusion.9
  139.9 3.7 %fusion.2 = f32[128,2048]{1,0:T(8,128)S(1)} fusion(bf16[128,1024]{0,1:T(8,128)(2,1)S(1)} %bitcast.74, bf16[2048,1280]{1,0:T(8,128)(2,1)} %all-gather.2.cloned.1.call-done), kind=kOutput, calls=%fused_computation.2 | convolution fusion | flops 536870912 | bytes 5505024 | tf_op jit(solution)/shard_map/dot_general | solution.py:114
  143.9 27.3 %all_to_all.16 = f32[2,128,2048]{2,1,0:T(8,128)S(1)} all-to-all(f32[2,128,2048]{2,1,0:T(8,128)S(1)} %broadcast_in_dim.16), channel_id=1, replica_groups=mesh['dp_0'=8,'dp_1'=4,'dp_2'=2,'dp_3'=2,'tensor'=2] {'tensor'}, dimensions={0} | all-to-all | bytes 4194304 | tf_op jit(solution)/shard_map/all_to_all | solution.py:29
  171.2 1.2 reduce_sum.144
  172.5 3.2 %fusion.6 = bf16[128,1024]{1,0:T(8,128)(2,1)S(1)} fusion(bf16[2048,1280]{1,0:T(8,128)(2,1)} %all-gather.2.cloned.1.call-done, f32[128,2048]{1,0:T(8,128)} %reduce_sum.144, bf16[128,2048]{1,0:T(8,128)(2,1)S(1)} %copy-done.1), kind=kOutput, calls=%fused_computation.9 | convolution fusion | flops 537788416 | bytes 6029312 | tf_op jit(solution)/shard_map/dot_general | solution.py:121
  176.7 1.9 copy.34
  178.6 1.8 copy.35
  180.4 6.2 %all_to_all.15 = f32[2,64,16,256]{3,2,1,0:T(8,128)S(1)} all-to-all(f32[2,64,16,256]{3,2,1,0:T(8,128)S(1)} %copy.35), channel_id=1, replica_groups=mesh['dp_0'=8,'dp_1'=4,'dp_2'=2,'dp_3'=2,'tensor'=2] {'dp_3'}, dimensions={0} | all-to-all | bytes 4194304 | tf_op jit(solution)/shard_map/all_to_all | solution.py:44
  186.6 1.3 reduce_sum.152
  187.9 7.8 %all-to-all-start.2 = ((f32[64,16,256]{2,1,0:T(8,128)}), f32[64,16,256]{2,1,0:T(8,128)S(1)}, u32[]{:S(2)}, u32[]{:S(2)}) async-start(f32[64,16,256]{2,1,0:T(8,128)} %reduce_sum.152), calls=%async_computation.2 | async-start | bytes 2097152 | tf_op jit(solution)/shard_map/all_to_all | solution.py:51
  195.7 0.6 dynamic-slice
  196.3 2.1 multiply_reduce_fusion
  199.1 0.8 dynamic-update-slice
  199.8 23.6 %all-to-all-done.2 = f32[64,16,256]{2,1,0:T(8,128)S(1)} async-done(((f32[64,16,256]{2,1,0:T(8,128)}), f32[64,16,256]{2,1,0:T(8,128)S(1)}, u32[]{:S(2)}, u32[]{:S(2)}) %all-to-all-start.2) | async-done | bytes 1048608 | tf_op jit(solution)/shard_map/all_to_all | solution.py:51
  223.5 0.6 multiply_reduce_fusion.1
  224.1 1.4 dynamic-update-slice.5
  225.5 0.6 dynamic-slice.1
  226.1 13.6 %all-reduce.10 = (f32[8]{0:T(128)S(1)}, f32[8]{0:T(128)S(1)}) all-reduce(f32[8]{0:T(128)S(1)} %dynamic-update-slice, f32[8]{0:T(128)S(1)} %dynamic-update-slice.5), channel_id=1, replica_groups=mesh['dp_0'=8,'dp_1'=4,'dp_2'=2,'dp_3'=2,'tensor'=2] {'dp_0'}, use_global_device_ids=true, to_apply=%add | all-reduce | flops 16 | bytes 128
  239.7 0.6 reduce_sum.155
  240.3 0.6 reduce_sum.146
  240.9 1.4 dynamic-update-slice.6
  242.3 1.4 dynamic-update-slice.1
  244.3 6.8 %all-reduce.11 = (f32[4]{0:T(128)S(1)}, f32[4]{0:T(128)S(1)}) all-reduce(f32[4]{0:T(128)S(1)} %dynamic-update-slice.1, f32[4]{0:T(128)S(1)} %dynamic-update-slice.6), channel_id=1, replica_groups=mesh['dp_0'=8,'dp_1'=4,'dp_2'=2,'dp_3'=2,'tensor'=2] {'dp_1'}, use_global_device_ids=true, to_apply=%add.1 | all-reduce | flops 8 | bytes 64
  251.2 0.6 reduce_sum.156
  251.8 0.6 reduce_sum.147
  252.4 1.4 dynamic-update-slice.7
  253.8 1.4 dynamic-update-slice.2
  255.7 5.3 %all-reduce.14 = (f32[2]{0:T(128)S(1)}, f32[2]{0:T(128)S(1)}) all-reduce(f32[2]{0:T(128)S(1)} %dynamic-update-slice.2, f32[2]{0:T(128)S(1)} %dynamic-update-slice.7), channel_id=1, replica_groups=mesh['dp_0'=8,'dp_1'=4,'dp_2'=2,'dp_3'=2,'tensor'=2] {'dp_2'}, use_global_device_ids=true, to_apply=%add.2 | all-reduce | flops 4 | bytes 32
  261.0 0.6 reduce_sum.157
  261.6 0.6 reduce_sum.148
  262.2 1.4 dynamic-update-slice.8
  263.6 1.4 dynamic-update-slice.3
  265.6 11.3 %all-reduce.13 = (f32[2]{0:T(128)S(1)}, f32[2]{0:T(128)S(1)}) all-reduce(f32[2]{0:T(128)S(1)} %dynamic-update-slice.3, f32[2]{0:T(128)S(1)} %dynamic-update-slice.8), channel_id=1, replica_groups=mesh['dp_0'=8,'dp_1'=4,'dp_2'=2,'dp_3'=2,'tensor'=2] {'dp_3'}, use_global_device_ids=true, to_apply=%add.3 | all-reduce | flops 4 | bytes 32
  276.9 0.6 reduce_sum.158
  277.5 0.6 reduce_sum.149
  278.1 1.4 dynamic-update-slice.9
  279.5 1.4 dynamic-update-slice.4
  280.9 3.8 %all-reduce.12 = (f32[2]{0:T(128)S(1)}, f32[2]{0:T(128)S(1)}) all-reduce(f32[2]{0:T(128)S(1)} %dynamic-update-slice.4, f32[2]{0:T(128)S(1)} %dynamic-update-slice.9), channel_id=1, replica_groups=mesh['dp_0'=8,'dp_1'=4,'dp_2'=2,'dp_3'=2,'tensor'=2] {'tensor'}, use_global_device_ids=true, to_apply=%add.4 | all-reduce | flops 4 | bytes 32
  284.7 0.6 reduce_sum.159
  286.0 0.6 reduce_sum.150
  287.3 0.6 multiply_add_fusion
  (49 shorter events, 4.0 us)
Async XLA Ops:
  7.2 2.9 copy-start
  7.2 129.9 %all-gather.2.cloned.1.call-start = ((), (), s32[]{:S(2)}) async-start(), calls=%async_computation.3 | async-start | bytes 5283840 | tf_op jit(solution)/shard_map/all_gather | solution.py:23
  143.9 28.6 %copy-start.1 = (bf16[128,2048]{1,0:T(8,128)(2,1)S(1)}, bf16[128,2048]{1,0:T(8,128)(2,1)}, u32[]{:S(2)}) copy-start(bf16[128,2048]{1,0:T(8,128)(2,1)} %param.12) | copy-start | bytes 1572868
  172.5 3.4 %copy-start.5 = (f32[8]{0:T(128)S(1)}, f32[8]{0:T(128)}, u32[]{:S(2)}) copy-start(f32[8]{0:T(128)} %param.21) | copy-start | bytes 100
  180.4 15.3 %copy-start.10 = (u32[256]{0:T(256)S(1)}, u32[256]{0:T(256)}, u32[]{:S(2)}) copy-start(u32[256]{0:T(256)} %constant.46) | copy-start | bytes 3076
  186.6 39.0 %copy-start.9 = (u32[256]{0:T(256)S(1)}, u32[256]{0:T(256)}, u32[]{:S(2)}) copy-start(u32[256]{0:T(256)} %constant.51) | copy-start | bytes 3076
  186.6 57.2 %copy-start.8 = (u32[256]{0:T(256)S(1)}, u32[256]{0:T(256)}, u32[]{:S(2)}) copy-start(u32[256]{0:T(256)} %constant.56) | copy-start | bytes 3076
  186.6 68.6 %copy-start.7 = (u32[256]{0:T(256)S(1)}, u32[256]{0:T(256)}, u32[]{:S(2)}) copy-start(u32[256]{0:T(256)} %constant.61) | copy-start | bytes 3076
  186.6 78.5 %copy-start.6 = (u32[256]{0:T(256)S(1)}, u32[256]{0:T(256)}, u32[]{:S(2)}) copy-start(u32[256]{0:T(256)} %constant.66) | copy-start | bytes 3076
  186.6 100.7 %copy-start.2 = (f32[16,256]{1,0:T(8,128)S(1)}, f32[16,256]{1,0:T(8,128)}, u32[]{:S(2)}) copy-start(f32[16,256]{1,0:T(8,128)} %param.13) | copy-start | bytes 49156
  186.6 100.7 %copy-start.3 = (f32[16,256]{1,0:T(8,128)S(1)}, f32[16,256]{1,0:T(8,128)}, u32[]{:S(2)}) copy-start(f32[16,256]{1,0:T(8,128)} %param.15) | copy-start | bytes 49156
  186.6 100.7 %copy-start.4 = (f32[16,256]{1,0:T(8,128)S(1)}, f32[16,256]{1,0:T(8,128)}, u32[]{:S(2)}) copy-start(f32[16,256]{1,0:T(8,128)} %param.16) | copy-start | bytes 49156
  187.9 35.6 %all-to-all-start.2 = ((f32[64,16,256]{2,1,0:T(8,128)}), f32[64,16,256]{2,1,0:T(8,128)S(1)}, u32[]{:S(2)}, u32[]{:S(2)}) async-start(f32[64,16,256]{2,1,0:T(8,128)} %reduce_sum.152), calls=%async_computation.2 | async-start | bytes 2097152 | tf_op jit(solution)/shard_map/all_to_all | solution.py:51
Sparse Core Ops, SparseCore 0:
  11.6 125.4 all-gather.1
